TPU v7x, 32 devices: a whole 2x2x4 slice. The times are simulated.
32 devices in a mesh: dp: 4 (over y, x), fsdp: 8 (over z, core).
Axes of the slice: x: 2, y: 2, z: 4, core: 2. Of those that a mesh axis runs over, the one named last changes fastest.
Arguments:
- tokens: bfloat16 [32768, 768], P(('dp', 'fsdp')), may hold values from -6 to 6
- cotangent: bfloat16 [32768, 768], P(('dp', 'fsdp')), may hold values from -6 to 6
- lengths: int32 [64], P(('dp', 'fsdp')), may hold values from 128 to 512, as said below
- mb_count: int32 [4], replicated, may hold values from 1 to 2, as said below
- query_weight: bfloat16 [768, 768], P('fsdp'), may hold values from -0.21875 to 0.21875
- query_bias: bfloat16 [768], P('fsdp'), may hold values from -1.5 to 1.5
- key_weight: bfloat16 [768, 768], P('fsdp'), may hold values from -0.21875 to 0.21875
- value_weight: bfloat16 [768, 768], P('fsdp'), may hold values from -0.21875 to 0.21875
- value_bias: bfloat16 [768], P('fsdp'), may hold values from -1.5 to 1.5
- output_weight: bfloat16 [768, 768], P('fsdp'), may hold values from -1.75 to 1.75
- output_bias: bfloat16 [768], P('fsdp'), may hold values from -1.5 to 1.5
- first_gain: bfloat16 [768], P('fsdp'), may hold values from 0.5 to 1.5
- first_shift: bfloat16 [768], P('fsdp'), may hold values from -1.5 to 1.5
- up_weight: bfloat16 [768, 3072], P('fsdp'), may hold values from -0.21875 to 0.21875
- up_bias: bfloat16 [3072], P('fsdp'), may hold values from -1.5 to 1.5
- down_weight: bfloat16 [3072, 768], P('fsdp'), may hold values from -0.109375 to 0.109375
- down_bias: bfloat16 [768], P('fsdp'), may hold values from -1.5 to 1.5
- second_gain: bfloat16 [768], P('fsdp'), may hold values from 0.5 to 1.5
- second_shift: bfloat16 [768], P('fsdp'), may hold values from -1.5 to 1.5
Outputs:
- layer_out: bfloat16 [32768, 768], P(('dp', 'fsdp'))
- tokens_grad: bfloat16 [32768, 768], P(('dp', 'fsdp'))
- query_weight_grad: float32 [768, 768], P('fsdp')
- query_bias_grad: float32 [768], P('fsdp')
- key_weight_grad: float32 [768, 768], P('fsdp')
- value_weight_grad: float32 [768, 768], P('fsdp')
- value_bias_grad: float32 [768], P('fsdp')
- output_weight_grad: float32 [768, 768], P('fsdp')
- output_bias_grad: float32 [768], P('fsdp')
- first_gain_grad: float32 [768], P('fsdp')
- first_shift_grad: float32 [768], P('fsdp')
- up_weight_grad: float32 [768, 3072], P('fsdp')
- up_bias_grad: float32 [3072], P('fsdp')
- down_weight_grad: float32 [3072, 768], P('fsdp')
- down_bias_grad: float32 [768], P('fsdp')
- second_gain_grad: float32 [768], P('fsdp')
- second_shift_grad: float32 [768], P('fsdp')
Inputs may be any that keep to these rules, and one draw needn't show every extreme that they name: `lengths`: keys at positions at or past a sequence's length are padding; some sequence has all 512 keys valid and some has 128. Data group g runs slots 0 .. mb_count[g] - 1 of each of its devices; some group runs all 2 and some runs one.
All inputs are finite; a program needn't handle non-finite values.
Results may differ from a plain program's by a relative error of at most 0.02.
Values may be sent and summed in bfloat16 or wider, within the bound.
A program may use at most 144 MiB of HBM per device.

v0:
```python
import jax
import jax.numpy as jnp
from jax import lax
from jax.sharding import PartitionSpec as P

HEADS = 12
MB_CAP = 2


norm_epsilon = 1e-05


def for_sending(shard):

    def short(part):
        return part.astype(jnp.bfloat16) if part.dtype == jnp.float32 else part

    return jax.tree.map(short, shard)


def gelu_exact(values):
    return jax.nn.gelu(values, approximate=False)


def layer_norm(hidden, gain, shift):
    centre = hidden - jnp.mean(hidden, axis=-1, keepdims=True)
    inverse = lax.rsqrt(jnp.mean(centre * centre, axis=-1, keepdims=True) + norm_epsilon)
    normed = centre * inverse
    return (normed * gain.astype(jnp.float32) + shift.astype(jnp.float32), normed, inverse)


def norm_backward(grad_out, normed, inverse, gain):
    scaled = grad_out * gain.astype(jnp.float32)
    inner = scaled - jnp.mean(scaled, axis=-1, keepdims=True)
    inner = inner - normed * jnp.mean(scaled * normed, axis=-1, keepdims=True)
    return inverse * inner


def to_heads(values, seq_count, heads):
    width = values.shape[1]
    shaped = values.reshape(seq_count, -1, heads, width // heads)
    return jnp.transpose(shaped, (0, 2, 3, 1))


def from_heads(values):
    shaped = jnp.transpose(values, (0, 3, 1, 2))
    return shaped.reshape(-1, values.shape[1] * values.shape[2])


def masked_scores(query_cols, key_cols, length):
    factor = query_cols.shape[1] ** (-0.5)
    scores = (
        jnp.einsum("hdq,hdk->hqk", query_cols, key_cols, preferred_element_type=jnp.float32)
        * factor
    )
    visible = jnp.arange(key_cols.shape[2], dtype=jnp.int32) < length
    masked = jnp.where(visible[None, None, :], scores, -1000000000.0)
    return (masked, factor)


def attend_forward(query_cols, key_cols, value_cols, length):
    scores, factor = masked_scores(query_cols, key_cols, length)
    top = jnp.max(scores, axis=-1, keepdims=True)
    expo = jnp.exp(scores - top)
    total = jnp.sum(expo, axis=-1, keepdims=True)
    probs = (expo / total).astype(jnp.bfloat16)
    log_total = top[..., 0] + jnp.log(total[..., 0])
    context = jnp.einsum("hdk,hqk->hdq", value_cols, probs, preferred_element_type=jnp.float32)
    return (context.astype(jnp.bfloat16), log_total)


def attend_backward(query_cols, key_cols, value_cols, length, log_total, grad_cols):
    scores, factor = masked_scores(query_cols, key_cols, length)
    probs = jnp.exp(scores - log_total[..., None])
    grad_probs = jnp.einsum(
        "hdq,hdk->hqk", grad_cols, value_cols, preferred_element_type=jnp.float32
    )
    grad_values = jnp.einsum(
        "hqk,hdq->hdk", probs.astype(jnp.bfloat16), grad_cols, preferred_element_type=jnp.float32
    ).astype(jnp.bfloat16)
    delta = jnp.sum(grad_probs * probs, axis=-1, keepdims=True)
    grad_scores = (probs * (grad_probs - delta)).astype(jnp.bfloat16)
    grad_queries = (
        factor
        * jnp.einsum("hqk,hdk->hdq", grad_scores, key_cols, preferred_element_type=jnp.float32)
    ).astype(jnp.bfloat16)
    grad_keys = (
        factor
        * jnp.einsum("hqk,hdq->hdk", grad_scores, query_cols, preferred_element_type=jnp.float32)
    ).astype(jnp.bfloat16)
    return (grad_queries, grad_keys, grad_values)


def project(left, right):
    return jnp.dot(left, right, preferred_element_type=jnp.float32)


def project_back(left, right):
    return jnp.einsum("rc,dc->rd", left, right, preferred_element_type=jnp.float32)


def weight_grad(left, right):
    return jnp.einsum("rc,rd->cd", left, right, preferred_element_type=jnp.float32)


def column_sum(values):
    return jnp.sum(values.astype(jnp.float32), axis=0)


def slot_forward(rows, weights, seq_lengths, heads):
    (
        w_query,
        b_query,
        w_key,
        w_value,
        b_value,
        w_output,
        b_output,
        gain_one,
        shift_one,
        w_up,
        b_up,
        w_down,
        b_down,
        gain_two,
        shift_two,
    ) = weights
    seq_count = seq_lengths.shape[0]
    queries = (project(rows, w_query) + b_query.astype(jnp.float32)).astype(jnp.bfloat16)
    key_rows = project(rows, w_key).astype(jnp.bfloat16)
    value_rows = (project(rows, w_value) + b_value.astype(jnp.float32)).astype(jnp.bfloat16)
    query_cols = to_heads(queries, seq_count, heads)
    key_cols = to_heads(key_rows, seq_count, heads)
    value_cols = to_heads(value_rows, seq_count, heads)

    def one_sequence(item):
        return attend_forward(item[0], item[1], item[2], item[3])

    context_cols, log_total = lax.map(one_sequence, (query_cols, key_cols, value_cols, seq_lengths))
    context = from_heads(context_cols)
    first_sum = rows.astype(jnp.float32) + project(context, w_output) + b_output.astype(jnp.float32)
    middle, normed_one, inverse_one = layer_norm(first_sum, gain_one, shift_one)
    middle_low = middle.astype(jnp.bfloat16)
    upper = project(middle_low, w_up) + b_up.astype(jnp.float32)
    active = gelu_exact(upper).astype(jnp.bfloat16)
    second_sum = middle + project(active, w_down) + b_down.astype(jnp.float32)
    result, normed_two, inverse_two = layer_norm(second_sum, gain_two, shift_two)
    saved = (
        query_cols,
        key_cols,
        value_cols,
        log_total,
        context,
        normed_one,
        inverse_one,
        middle_low,
        upper,
        active,
        normed_two,
        inverse_two,
    )
    return (result, saved)


def slot_backward(rows, grad_out, saved, weights, seq_lengths, heads):
    (
        w_query,
        b_query,
        w_key,
        w_value,
        b_value,
        w_output,
        b_output,
        gain_one,
        shift_one,
        w_up,
        b_up,
        w_down,
        b_down,
        gain_two,
        shift_two,
    ) = weights
    (
        query_cols,
        key_cols,
        value_cols,
        log_total,
        context,
        normed_one,
        inverse_one,
        middle_low,
        upper,
        active,
        normed_two,
        inverse_two,
    ) = saved
    seq_count = seq_lengths.shape[0]
    gain_two_grad = jnp.sum(grad_out * normed_two, axis=0)
    shift_two_grad = jnp.sum(grad_out, axis=0)
    grad_second = norm_backward(grad_out, normed_two, inverse_two, gain_two)
    grad_down = grad_second.astype(jnp.bfloat16)
    down_bias_grad = column_sum(grad_down)
    down_weight_grad = weight_grad(active, grad_down)
    grad_active = project_back(grad_down, w_down)
    gelu_value, gelu_pull = jax.vjp(gelu_exact, upper)
    grad_upper = gelu_pull(grad_active)[0].astype(jnp.bfloat16)
    up_bias_grad = column_sum(grad_upper)
    up_weight_grad = weight_grad(middle_low, grad_upper)
    grad_middle = grad_second + project_back(grad_upper, w_up)
    gain_one_grad = jnp.sum(grad_middle * normed_one, axis=0)
    shift_one_grad = jnp.sum(grad_middle, axis=0)
    grad_first = norm_backward(grad_middle, normed_one, inverse_one, gain_one)
    grad_branch = grad_first.astype(jnp.bfloat16)
    output_bias_grad = column_sum(grad_branch)
    output_weight_grad = weight_grad(context, grad_branch)
    grad_context = project_back(grad_branch, w_output).astype(jnp.bfloat16)
    grad_cols = to_heads(grad_context, seq_count, heads)

    def one_sequence(item):
        return attend_backward(item[0], item[1], item[2], item[3], item[4], item[5])

    grad_query_cols, grad_key_cols, grad_value_cols = lax.map(
        one_sequence, (query_cols, key_cols, value_cols, seq_lengths, log_total, grad_cols)
    )
    grad_queries = from_heads(grad_query_cols)
    grad_keys = from_heads(grad_key_cols)
    grad_values = from_heads(grad_value_cols)
    grads = (
        weight_grad(rows, grad_queries),
        column_sum(grad_queries),
        weight_grad(rows, grad_keys),
        weight_grad(rows, grad_values),
        column_sum(grad_values),
        output_weight_grad,
        output_bias_grad,
        gain_one_grad,
        shift_one_grad,
        up_weight_grad,
        up_bias_grad,
        down_weight_grad,
        down_bias_grad,
        gain_two_grad,
        shift_two_grad,
    )
    grad_rows = grad_first + project_back(grad_queries, w_query) + project_back(grad_keys, w_key)
    grad_rows = grad_rows + project_back(grad_values, w_value)
    return (grad_rows.astype(jnp.bfloat16), grads)


def local(
    tokens,
    cotangent,
    lengths,
    mb_count,
    query_weight,
    query_bias,
    key_weight,
    value_weight,
    value_bias,
    output_weight,
    output_bias,
    first_gain,
    first_shift,
    up_weight,
    up_bias,
    down_weight,
    down_bias,
    second_gain,
    second_shift,
):
    shards = (
        query_weight,
        query_bias,
        key_weight,
        value_weight,
        value_bias,
        output_weight,
        output_bias,
        first_gain,
        first_shift,
        up_weight,
        up_bias,
        down_weight,
        down_bias,
        second_gain,
        second_shift,
    )
    group_size = lax.axis_size("fsdp")
    slot_rows = tokens.shape[0] // MB_CAP
    slot_seqs = lengths.shape[0] // MB_CAP
    group_count = mb_count[lax.axis_index("dp")]
    totals = tuple(
        (jnp.zeros((group_size * item.shape[0],) + item.shape[1:], jnp.float32) for item in shards)
    )
    results = []
    input_grads = []
    for slot_index in range(MB_CAP):
        gathered = (
            lax.all_gather(shards[0], "fsdp", axis=0, tiled=True),
            lax.all_gather(shards[1], "fsdp", axis=0, tiled=True),
            lax.all_gather(shards[2], "fsdp", axis=0, tiled=True),
            lax.all_gather(shards[3], "fsdp", axis=0, tiled=True),
            lax.all_gather(shards[4], "fsdp", axis=0, tiled=True),
            lax.all_gather(shards[5], "fsdp", axis=0, tiled=True),
            lax.all_gather(shards[6], "fsdp", axis=0, tiled=True),
            lax.all_gather(shards[7], "fsdp", axis=0, tiled=True),
            lax.all_gather(shards[8], "fsdp", axis=0, tiled=True),
            lax.all_gather(shards[9], "fsdp", axis=0, tiled=True),
            lax.all_gather(shards[10], "fsdp", axis=0, tiled=True),
            lax.all_gather(shards[11], "fsdp", axis=0, tiled=True),
            lax.all_gather(shards[12], "fsdp", axis=0, tiled=True),
            lax.all_gather(shards[13], "fsdp", axis=0, tiled=True),
            lax.all_gather(shards[14], "fsdp", axis=0, tiled=True),
        )
        rows = tokens[slot_index * slot_rows : (slot_index + 1) * slot_rows]
        seq_lengths = lengths[slot_index * slot_seqs : (slot_index + 1) * slot_seqs]
        result, saved = slot_forward(rows, gathered, seq_lengths, HEADS)
        results.append(result.astype(jnp.bfloat16))
        grad_out = cotangent[slot_index * slot_rows : (slot_index + 1) * slot_rows].astype(
            jnp.float32
        )

        def run_backward(carried):
            grad_rows, grads = slot_backward(rows, grad_out, saved, gathered, seq_lengths, HEADS)
            return (grad_rows, tuple((total + piece for total, piece in zip(carried, grads))))

        def skip_backward(carried):
            return (jnp.zeros_like(rows), carried)

        grad_rows, totals = lax.cond(slot_index < group_count, run_backward, skip_backward, totals)
        input_grads.append(grad_rows)
    pieces = jax.tree.map(
        lambda part: part.astype(jnp.float32),
        lax.psum_scatter(for_sending(totals), "fsdp", scatter_dimension=0, tiled=True),
    )
    summed = jax.tree.map(
        lambda part: part.astype(jnp.float32), lax.psum(for_sending(pieces), "dp")
    )
    return (jnp.concatenate(results, axis=0), jnp.concatenate(input_grads, axis=0)) + tuple(summed)


def solution(mesh):
    return jax.shard_map(
        local,
        mesh=mesh,
        in_specs=(
            P(("dp", "fsdp"), None),
            P(("dp", "fsdp"), None),
            P(("dp", "fsdp")),
            P(),
            P("fsdp", None),
            P("fsdp"),
            P("fsdp", None),
            P("fsdp", None),
            P("fsdp"),
            P("fsdp", None),
            P("fsdp"),
            P("fsdp"),
            P("fsdp"),
            P("fsdp", None),
            P("fsdp"),
            P("fsdp", None),
            P("fsdp"),
            P("fsdp"),
            P("fsdp"),
        ),
        out_specs=(
            P(("dp", "fsdp"), None),
            P(("dp", "fsdp"), None),
            P("fsdp", None),
            P("fsdp"),
            P("fsdp", None),
            P("fsdp", None),
            P("fsdp"),
            P("fsdp", None),
            P("fsdp"),
            P("fsdp"),
            P("fsdp"),
            P("fsdp", None),
            P("fsdp"),
            P("fsdp", None),
            P("fsdp"),
            P("fsdp"),
            P("fsdp"),
        ),
        check_vma=False,
    )
```

profile of v0, /device:TPU:0, one launch (start us, length us, event | category | flops | bytes accessed | tf_op | source)
XLA Modules:
  0.0 763.6 jit_solution(17119618371949956671)
XLA Ops:
  21.6 31.4 %all-reduce.18 = (bf16[768]{0:T(1024)(128)(2,1)S(1)}, bf16[768]{0:T(1024)(128)(2,1)S(1)}, bf16[768]{0:T(1024)(128)(2,1)S(1)}, bf16[768]{0:T(1024)(128)(2,1)S(1)}...) all-reduce(bf16[768]{0:T(1024)(128)(2,1)S(1)} %dynamic-update-slice, ...), channel_id=1, replica_groups=mesh['dp'=4,'fsdp'=8] {'fsdp'}, use_global_device_ids=true, to_apply=%add | all-reduce | flops 5376 | bytes 21504
  55.7 12.7 %all-gather = bf16[8,1,384]{2,1,0:T(2,128)(2,1)S(1)} all-gather(bf16[1,1,384]{2,1,0:T(2,128)(2,1)S(1)} %reshape.281), channel_id=1, replica_groups=mesh['dp'=4,'fsdp'=8] {'fsdp'}, dimensions={0}, use_global_device_ids=true | all-gather | bytes 6912 | tf_op jit(solution)/shard_map/all_gather | solution.py:309
  96.6 11.0 %all-gather.14.cloned.1.call-done = bf16[768,768]{1,0:T(8,128)(2,1)} async-done(((bf16[96,768]{1,0:T(8,128)(2,1)}), bf16[768,768]{1,0:T(8,128)(2,1)}) %all-gather.14.cloned.1.call-update) | async-done | bytes 1179664 | tf_op jit(solution)/shard_map/all_gather | solution.py:304
  136.5 23.4 %all-gather.16.cloned.1.call-done = bf16[768,3072]{1,0:T(8,128)(2,1)} async-done(((bf16[96,3072]{1,0:T(8,128)(2,1)}), bf16[768,3072]{1,0:T(8,128)(2,1)}) %all-gather.16.cloned.1.call-update) | async-done | bytes 4718608 | tf_op jit(solution)/shard_map/all_gather | solution.py:308
  160.0 18.8 %fusion.76 = (bf16[512,3072]{1,0:T(8,128)(2,1)}, f32[512,3072]{1,0:T(8,128)}) fusion(f32[3072]{0:T(1024)S(1)} %bitcast.279, bf16[512,768]{1,0:T(8,128)(2,1)} %get-tuple-element.852, bf16[768,3072]{1,0:T(8,128)(2,1)} %all-gather.16.cloned.1.call-done), kind=kOutput, calls=%fused_computation.162 | convolution fusion | flops 2519728128 | bytes 14954496 | tf_op jit(solution)/shard_map/dot_general | solution.py:95
  178.7 32.7 %all-gather.18.cloned.1.call-done = bf16[3072,768]{1,0:T(8,128)(2,1)} async-done(((bf16[384,768]{1,0:T(8,128)(2,1)}), bf16[3072,768]{1,0:T(8,128)(2,1)}) %all-gather.18.cloned.1.call-update) | async-done | bytes 4718608 | tf_op jit(solution)/shard_map/all_gather | solution.py:310
  218.2 18.2 %fusion.79 = (bf16[512,3072]{1,0:T(8,128)(2,1)S(1)}, f32[512,3072]{1,0:T(8,128)}) fusion(f32[3072]{0:T(1024)S(1)} %bitcast.280, bf16[512,768]{1,0:T(8,128)(2,1)S(1)} %copy-done.50, bf16[768,3072]{1,0:T(8,128)(2,1)S(1)} %copy-done.97), kind=kOutput, calls=%fused_computation.165 | convolution fusion | flops 2519728128 | bytes 14954496 | tf_op jit(solution)/shard_map/dot_general | solution.py:95
  241.4 90.8 %conditional.2 = (bf16[512,768]{1,0:T(8,128)(2,1)}, f32[768,768]{0,1:T(8,128)S(1)}, f32[768]{0:T(1024)S(1)}, f32[768,768]{0,1:T(8,128)}, f32[768,768]{0,1:T(8,12...) conditional(s32[]{:T(128)} %bitcast.104, () %tuple.36, ...), branch_computations={%region_12.13_spmd, %region_13.28_spmd} | conditional | flops 16691619840 | bytes 337698560 | solution.py:330
  249.7 17.9 %convert_reduce_fusion = (f32[3072]{0:T(1024)S(1)}, bf16[512,3072]{1,0:T(8,128)(2,1)S(1)}) fusion(f32[512,3072]{1,0:T(8,128)S(1)} %get-tuple-element.439, bf16[3072,768]{1,0:T(8,128)(2,1)S(1)} %get-tuple-element.440, f32[512,768]{1,0:T(8,128)S(1)} %get-tuple-element.845), kind=kOutput, calls=%fused_computation.10 | convolution fusion | flops 2532701184 | bytes 15740928 | tf_op jit(solution)/shard_map/cond/branch_1_fun/rc,dc->rd/dot_general | solution.py:99
  275.2 11.7 %multiply_reduce_fusion = (f32[12,512]{1,0:T(8,128)S(1)}, f32[12,512,512]{1,2,0:T(8,128)}) fusion(f32[12,512,512]{1,2,0:T(8,128)} %fusion.22, f32[12,512]{1,0:T(8,128)S(1)} %log_add_fusion, pred[512]{0:T(512)(128)(4,1)S(1)} %iota_compare_fusion, bf16[12,64,512]{2,1,0:T(8,128)(2,1)} %bitcast.259, bf16[1,12,64,512]{3,2,1,0:T(8,128)(2,1)S(1)} %copy-done.41), kind=kOutput, calls=%fused_computation.1 | convolution fusion | flops 418375680 | bytes 26788352 | tf_op jit(solution)/shard_map/cond/branch_1_fun/while/body/eval_jaxpr/hdq,hdk->hqk/dot_general | solution.py:75
  288.0 7.4 multiply_convert_fusion
  318.5 8.4 %convolution_bitcast_fusion.1 = f32[768,3072]{0,1:T(8,128)} fusion(bf16[512,3072]{1,0:T(8,128)(2,1)} %copy-done.106, bf16[512,768]{1,0:T(8,128)(2,1)} %get-tuple-element.456), kind=kOutput, calls=%fused_computation.29 | convolution fusion | flops 2415919104 | bytes 13369344 | tf_op jit(solution)/shard_map/cond/branch_1_fun/rc,rd->cd/dot_general | solution.py:103
  332.8 10.1 %conditional.3 = (bf16[512,768]{1,0:T(8,128)(2,1)}, f32[768,768]{0,1:T(8,128)S(1)}, f32[768]{0:T(1024)S(1)}, f32[768,768]{0,1:T(8,128)}, f32[768,768]{0,1:T(8,12...) conditional(s32[]{:T(128)} %bitcast.110, ...), branch_computations={%region_28.29_spmd, %region_29.44_spmd} | conditional | flops 16698708992 | bytes 455893312 | solution.py:330
  352.7 7.7 %copy.106 = bf16[768,3072]{1,0:T(8,128)(2,1)} copy(f32[768,3072]{0,1:T(8,128)} %get-tuple-element.589) | data formatting | bytes 14155776 | tf_op jit(solution)/shard_map/cond | solution.py:330
  360.5 7.7 %copy.107 = bf16[3072,768]{1,0:T(8,128)(2,1)} copy(f32[3072,768]{0,1:T(8,128)} %get-tuple-element.591) | data formatting | bytes 14155776 | tf_op jit(solution)/shard_map/cond | solution.py:330
  368.3 97.2 %reduce-scatter.7.cloned.1.call-done = bf16[96,768]{1,0:T(8,128)(2,1)} async-done(((bf16[768,768]{1,0:T(8,128)(2,1)}), bf16[96,768]{1,0:T(8,128)(2,1)}) %reduce-scatter.7.cloned.1.call-update) | async-done | bytes 147472 | tf_op jit(solution)/shard_map/reduce_scatter | solution.py:334
  465.5 34.1 %reduce-scatter.9.cloned.1.call-done = bf16[96,768]{1,0:T(8,128)(2,1)} async-done(((bf16[768,768]{1,0:T(8,128)(2,1)}), bf16[96,768]{1,0:T(8,128)(2,1)}) %reduce-scatter.9.cloned.1.call-update) | async-done | bytes 147472 | tf_op jit(solution)/shard_map/reduce_scatter | solution.py:334
  499.5 34.1 %reduce-scatter.11.cloned.1.call-done = bf16[96,768]{1,0:T(8,128)(2,1)} async-done(((bf16[768,768]{1,0:T(8,128)(2,1)}), bf16[96,768]{1,0:T(8,128)(2,1)}) %reduce-scatter.11.cloned.1.call-update) | async-done | bytes 147472 | tf_op jit(solution)/shard_map/reduce_scatter | solution.py:334
  533.6 34.0 %reduce-scatter.13.cloned.1.call-done = bf16[96,768]{1,0:T(8,128)(2,1)} async-done(((bf16[768,768]{1,0:T(8,128)(2,1)}), bf16[96,768]{1,0:T(8,128)(2,1)}) %reduce-scatter.13.cloned.1.call-update) | async-done | bytes 147472 | tf_op jit(solution)/shard_map/reduce_scatter | solution.py:334
  567.6 55.4 %reduce-scatter.15.cloned.1.call-done = bf16[96,3072]{1,0:T(8,128)(2,1)} async-done(((bf16[768,3072]{1,0:T(8,128)(2,1)}), bf16[96,3072]{1,0:T(8,128)(2,1)}) %reduce-scatter.15.cloned.1.call-update) | async-done | bytes 589840 | tf_op jit(solution)/shard_map/reduce_scatter | solution.py:334
  623.0 55.5 %reduce-scatter.17.cloned.1.call-done = bf16[384,768]{1,0:T(8,128)(2,1)} async-done(((bf16[3072,768]{1,0:T(8,128)(2,1)}), bf16[384,768]{1,0:T(8,128)(2,1)}) %reduce-scatter.17.cloned.1.call-update) | async-done | bytes 589840 | tf_op jit(solution)/shard_map/reduce_scatter | solution.py:334
  680.2 26.0 %all-reduce.17 = (bf16[768]{0:T(1024)(128)(2,1)S(1)}, bf16[768]{0:T(1024)(128)(2,1)S(1)}, bf16[768]{0:T(1024)(128)(2,1)S(1)}, bf16[768]{0:T(1024)(128)(2,1)S(1)}...) all-reduce(bf16[768]{0:T(1024)(128)(2,1)S(1)} %dynamic-update-slice, ...), channel_id=1, replica_groups=mesh['dp'=4,'fsdp'=8] {'fsdp'}, use_global_device_ids=true, to_apply=%add.7 | all-reduce | flops 9984 | bytes 39936
  706.9 10.0 %all-reduce.19 = (bf16[96]{0:T(256)(128)(2,1)S(1)}, bf16[96]{0:T(256)(128)(2,1)S(1)}, bf16[96]{0:T(256)(128)(2,1)S(1)}, bf16[96]{0:T(256)(128)(2,1)S(1)}, bf16[9...) all-reduce(bf16[96]{0:T(256)(128)(2,1)S(1)} %dynamic-slice.17, ...), channel_id=1, replica_groups=mesh['dp'=4,'fsdp'=8] {'dp'}, use_global_device_ids=true, to_apply=%region_47.48 | all-reduce | flops 1152 | bytes 4608 | tf_op jit(solution)/shard_map/psum | solution.py:337
  726.1 19.6 %all-reduce.23.cloned.1.call-done = (bf16[96,768]{1,0:T(8,128)(2,1)}, bf16[96,768]{1,0:T(8,128)(2,1)}, bf16[96,768]{1,0:T(8,128)(2,1)}, bf16[96,768]{1,0:T(8,128...) async-done(((bf16[96,768]{1,0:T(8,128)(2,1)}, bf16[96,768]{1,0:T(8,128)(2,1)}, bf16[96,768]{1,0:T(8,128)(2,1)}, bf16[96,768]{1,0:T(8,128)(2,1)}, ...) | async-done | bytes 1769488 | tf_op jit(solution)/shard_map/psum | solution.py:337
  (335 shorter events, 160.2 us)
Async XLA Ops:
  7.2 66.0 %all-gather.8.cloned.1.call-start = ((), (), s32[]{:S(2)}) async-start(), calls=%async_computation.6 | async-start | bytes 1327104 | tf_op jit(solution)/shard_map/all_gather | solution.py:302
  7.9 67.7 %all-gather.10.cloned.1.call-start = ((), (), s32[]{:S(2)}) async-start(), calls=%async_computation.7 | async-start | bytes 1327104 | tf_op jit(solution)/shard_map/all_gather | solution.py:299
  8.7 75.0 %all-gather.12.cloned.1.call-start = ((), (), s32[]{:S(2)}) async-start(), calls=%async_computation.8 | async-start | bytes 1327104 | tf_op jit(solution)/shard_map/all_gather | solution.py:301
  9.4 98.2 %all-gather.14.cloned.1.call-start = ((), (), s32[]{:S(2)}) async-start(), calls=%async_computation.9 | async-start | bytes 1327104 | tf_op jit(solution)/shard_map/all_gather | solution.py:304
  10.0 150.0 %all-gather.16.cloned.1.call-start = ((), (), s32[]{:S(2)}) async-start(), calls=%async_computation.10 | async-start | bytes 5308416 | tf_op jit(solution)/shard_map/all_gather | solution.py:308
  10.6 200.9 %all-gather.18.cloned.1.call-start = ((), (), s32[]{:S(2)}) async-start(), calls=%async_computation.11 | async-start | bytes 5308416 | tf_op jit(solution)/shard_map/all_gather | solution.py:310
  11.2 454.3 %reduce-scatter.7.cloned.1.call-start = ((), (), s32[]{:S(2)}) async-start(), calls=%async_computation.12 | async-start | bytes 1327104 | tf_op jit(solution)/shard_map/reduce_scatter | solution.py:334
  136.5 99.9 %copy-start.30 = (f32[512,768]{1,0:T(8,128)}, f32[512,768]{1,0:T(8,128)S(1)}, u32[]{:S(2)}) copy-start(f32[512,768]{1,0:T(8,128)S(1)} %get-tuple-element.889) | copy-start | bytes 4718596
  344.4 155.2 %reduce-scatter.9.cloned.1.call-start = ((), (), s32[]{:S(2)}) async-start(), calls=%async_computation.13 | async-start | bytes 1327104 | tf_op jit(solution)/shard_map/reduce_scatter | solution.py:334
  347.1 186.5 %reduce-scatter.11.cloned.1.call-start = ((), (), s32[]{:S(2)}) async-start(), calls=%async_computation.14 | async-start | bytes 1327104 | tf_op jit(solution)/shard_map/reduce_scatter | solution.py:334
  349.9 217.7 %reduce-scatter.13.cloned.1.call-start = ((), (), s32[]{:S(2)}) async-start(), calls=%async_computation.15 | async-start | bytes 1327104 | tf_op jit(solution)/shard_map/reduce_scatter | solution.py:334
  352.6 270.3 %reduce-scatter.15.cloned.1.call-start = ((), (), s32[]{:S(2)}) async-start(), calls=%async_computation.16 | async-start | bytes 5308416 | tf_op jit(solution)/shard_map/reduce_scatter | solution.py:334
  360.4 318.1 %reduce-scatter.17.cloned.1.call-start = ((), (), s32[]{:S(2)}) async-start(), calls=%async_computation.17 | async-start | bytes 5308416 | tf_op jit(solution)/shard_map/reduce_scatter | solution.py:334
  368.1 311.7 %copy-start.105 = (bf16[96]{0:T(256)(128)(2,1)S(1)}, bf16[96]{0:T(256)(128)(2,1)}, u32[]{:S(2)}) copy-start(bf16[96]{0:T(256)(128)(2,1)} %param.41) | copy-start | bytes 580
  368.1 312.0 %copy-start.70 = (f32[768]{0:T(1024)S(1)}, f32[768]{0:T(1024)}, u32[]{:S(2)}) copy-start(f32[768]{0:T(1024)} %get-tuple-element.592) | copy-start | bytes 9220
  368.1 312.0 %copy-start.74 = (f32[768]{0:T(1024)S(1)}, f32[768]{0:T(1024)}, u32[]{:S(2)}) copy-start(f32[768]{0:T(1024)} %get-tuple-element.593) | copy-start | bytes 9220
  368.1 312.1 %copy-start.78 = (f32[768]{0:T(1024)S(1)}, f32[768]{0:T(1024)}, u32[]{:S(2)}) copy-start(f32[768]{0:T(1024)} %get-tuple-element.594) | copy-start | bytes 9220
  368.1 353.5 %copy-start.11 = (f32[512,768]{1,0:T(8,128)S(1)}, f32[512,768]{1,0:T(8,128)}, u32[]{:S(2)}) copy-start(f32[512,768]{1,0:T(8,128)} %copy-done.10) | copy-start | bytes 4718596
  368.1 353.5 %copy-start.13 = (f32[512,768]{1,0:T(8,128)S(1)}, f32[512,768]{1,0:T(8,128)}, u32[]{:S(2)}) copy-start(f32[512,768]{1,0:T(8,128)} %copy-done.12) | copy-start | bytes 4718596
  368.2 353.5 %copy-start.80 = (f32[512]{0:T(512)S(1)}, f32[512]{0:T(512)}, u32[]{:S(2)}) copy-start(f32[512]{0:T(512)} %copy-done.79) | copy-start | bytes 6148
  368.2 353.5 %copy-start.82 = (f32[512]{0:T(512)S(1)}, f32[512]{0:T(512)}, u32[]{:S(2)}) copy-start(f32[512]{0:T(512)} %copy-done.81) | copy-start | bytes 6148
  368.2 353.5 %copy-start.84 = (f32[512]{0:T(512)S(1)}, f32[512]{0:T(512)}, u32[]{:S(2)}) copy-start(f32[512]{0:T(512)} %copy-done.83) | copy-start | bytes 6148
  368.2 353.5 %copy-start.86 = (f32[512]{0:T(512)S(1)}, f32[512]{0:T(512)}, u32[]{:S(2)}) copy-start(f32[512]{0:T(512)} %copy-done.85) | copy-start | bytes 6148
  368.2 377.5 %all-reduce.23.cloned.1.call-start = ((), (), s32[]{:S(2)}) async-start(), calls=%async_computation.18 | async-start | bytes 3538944 | tf_op jit(solution)/shard_map/psum | solution.py:337
  (71 other events, 990.4 us)
Sparse Core Ops, SparseCore 0:
  9.6 25.8 all-gather.7
  37.2 22.3 all-gather.9
  61.2 22.3 all-gather.11
  85.1 22.4 all-gather.13
  109.1 50.8 all-gather.15
  161.5 49.9 all-gather.17
  344.5 120.9 reduce-scatter.6
  468.3 31.1 reduce-scatter.8
  502.4 31.1 reduce-scatter.10
  536.3 31.2 reduce-scatter.12
  569.9 53.0 reduce-scatter.14
  625.1 53.3 reduce-scatter.16
  682.3 63.3 all-reduce.22
where the time goes:
time: 775 us; the launch traced here: 764 us
  waiting for transfers between devices  406 us (52%)
  matrix products  156 us (20%)
  blocking collectives  80.1 us (10%)
  local copies, waits for them, and re-layouts  47.2 us (6%)
  other arithmetic  44.7 us (6%)
  between operations  18.8 us (2%)
  loops' own time  9.85 us (1%)
    reduce_scatter x6, waiting for transfers between devices, local(): lax.psum_scatter(for_sending(totals), 'fsdp', scatter_dimension=0, tiled=...  310 us
    dot_general x12, matrix products, project(): return jnp.dot(left, right, preferred_element_type=jnp.float32)  65.3 us
    unnamed x2, blocking collectives  57.4 us
    all_gather x1, waiting for transfers between devices, local(): lax.all_gather(shards[11], 'fsdp', axis=0, tiled=True)  32.7 us
    dot_general x6, matrix products, project_back(): jnp.einsum('rc,dc->rd', left, right, preferred_element_type=jnp.float32)  27.2 us
    dot_general x6, matrix products, weight_grad(): jnp.einsum('rc,rd->cd', left, right, preferred_element_type=jnp.float32)  25.2 us
    cond x6, local copies, waits for them, and re-layouts, local(): lax.cond(slot_index < group_count, run_backward, skip_backward, totals)  24.9 us
    all_gather x1, waiting for transfers between devices, local(): lax.all_gather(shards[9], 'fsdp', axis=0, tiled=True)  23.4 us
  transfers between devices with their start and end apart: 13, of which 11 were waited for; matrix products, arithmetic and copies ran while one was open for 15% of the time, Pallas kernels for 0%

commit v1 on v0

v1 whole, which is shorter than its diff:
```python
import jax
import jax.numpy as jnp
from jax import lax
from jax.experimental import pallas as pl
from jax.experimental.pallas import tpu as pltpu
from jax.sharding import PartitionSpec as P

HEADS = 12
MB_CAP = 2
EPSILON = 1e-05
TILE = 256
BF = jnp.bfloat16
F32 = jnp.float32


def dot(a, b):
    return jnp.dot(a, b, preferred_element_type=F32)


def dot_t(a, b):
    return lax.dot_general(a, b, (((1,), (1,)), ((), ())), preferred_element_type=F32)


def t_dot(a, b):
    return lax.dot_general(a, b, (((0,), (0,)), ((), ())), preferred_element_type=F32)


def fold(x):
    return jnp.sum(x.reshape(x.shape[0] // 8, 8, x.shape[1]), axis=0)


def rows_of(i, size=TILE):
    return pl.ds(pl.multiple_of(i * size, size), size)


def lanes_of(i, size=128):
    return pl.ds(pl.multiple_of(i * size, size), size)


def split3(x):
    hi = x.astype(BF).astype(F32)
    mid = (x - hi).astype(BF).astype(F32)
    return hi, mid, x - hi - mid


class Body:
    def __init__(self, **refs):
        self.__dict__.update(refs)
        self.rows, self.width = self.tok.shape
        self.seqs = self.lens.shape[0]
        self.seq = self.rows // self.seqs
        self.pairs = self.width // 128
        self.ff_blocks = self.w_up.shape[0]
        self.tiles = self.rows // TILE
        self.factor = 64**-0.5
        self.base = self.factor * 1.4426950408889634

    def vec(self, i):
        return self.vectors[i : i + 1, :]

    def add_sum(self, slot, x, lanes=None):
        lanes = slice(None) if lanes is None else lanes
        self.sums[slot, :, lanes] += fold(x)

    def masks(self):
        lane = lax.broadcasted_iota(jnp.int32, (1, 128), 1)
        first = jnp.where(lane < 64, 1.0, 0.0)
        return (first.astype(BF), (1.0 - first).astype(BF)), lane

    def prepare(self):
        self.sums[...] = jnp.zeros_like(self.sums)
        self.lse[...] = jnp.zeros_like(self.lse)
        lane = lax.broadcasted_iota(jnp.int32, (self.seq, 128), 1)
        pos = lax.broadcasted_iota(jnp.int32, (self.seq, 128), 0)
        for s in range(self.seqs):
            hidden = jnp.where(pos < self.lens[s], 0.0, -1e9)
            for h in range(2):
                base = 64 * (1 - h)
                ext = jnp.where(lane == base, hidden, 0.0)
                ext = jnp.where((lane > base) & (lane < base + 4), 1.0, ext)
                self.key_ext[s, h] = ext.astype(BF)

    def qkv_tile(self, i):
        x = self.tok[rows_of(i), :]
        self.q[rows_of(i), :] = (dot(x, self.w_q[...]) + self.vec(0)).astype(BF)
        self.k[rows_of(i), :] = dot(x, self.w_k[...]).astype(BF)
        self.v[rows_of(i), :] = (dot(x, self.w_v[...]) + self.vec(1)).astype(BF)

    def attend(self, n):
        s, p = n // self.pairs, n % self.pairs
        masks, lane = self.masks()
        lanes = lanes_of(p)
        k, v = self.k[rows_of(s, self.seq), lanes], self.v[rows_of(s, self.seq), lanes]
        ones = jnp.ones((self.seq, 128), BF)
        chunk = min(TILE, self.seq)
        keys = [k * masks[h] + self.key_ext[s, h] for h in range(2)]
        vals = [jnp.concatenate([v * masks[h], ones * masks[h]], axis=1) for h in range(2)]
        for c in range(self.seq // chunk):
            rows = pl.ds(pl.multiple_of(s * self.seq + c * chunk, chunk), chunk)
            q = self.q[rows, lanes]
            acc, tops = 0.0, []
            for h in range(2):
                one = jnp.where(lane == 64 * (1 - h), 1.0, 0.0).astype(BF)
                scores = dot_t(q * masks[h] + one, keys[h]) * self.base
                top = jnp.max(scores, axis=-1, keepdims=True)
                acc = acc + dot(jnp.exp2(scores - top).astype(BF), vals[h])
                tops.append(top)
            total = acc[:, 128:]
            self.ctx[rows, lanes] = (acc[:, :128] / total).astype(BF)
            lse = jnp.where(lane < 64, tops[0], tops[1]) + jnp.log2(total)
            old = self.lse[rows, :]
            old = jnp.where(lane == 2 * p, lse[:, :1], old)
            self.lse[rows, :] = jnp.where(lane == 2 * p + 1, lse[:, 64:65], old)

    def first_norm(self, i):
        r = rows_of(i)
        x = self.tok[r, :].astype(F32) + dot(self.ctx[r, :], self.w_o[...]) + self.vec(2)
        x = x - jnp.mean(x, axis=-1, keepdims=True)
        inverse = lax.rsqrt(jnp.mean(x * x, axis=-1, keepdims=True) + EPSILON)
        normed = x * inverse
        mid = normed * self.vec(3) + self.vec(4)
        self.inv1[r, :] = jnp.broadcast_to(inverse, (TILE, 128))
        self.normed1[r, :] = normed.astype(BF)
        self.mid[r, :] = mid.astype(BF)
        self.gs[r, :] = mid + self.vec(5)

    def feed(self, j, i):
        r = rows_of(i)
        upper = dot(self.mid[r, :], self.w_up[j]) + self.vectors[pl.ds(8 + j, 1), :]
        cdf = 0.5 * lax.erf(upper * 0.7071067811865476) + 0.5
        self.active[j, r, :] = (upper * cdf).astype(BF)
        slope = cdf + upper * (0.3989422804014327 * jnp.exp2(upper * upper * -0.7213475204444817))
        self.slope[j, r, :] = slope.astype(BF)
        self.gs[r, :] += dot(self.active[j, r, :], self.w_down[j])

    def second_norm(self, i):
        r = rows_of(i)
        x = self.gs[r, :]
        x = x - jnp.mean(x, axis=-1, keepdims=True)
        inverse = lax.rsqrt(jnp.mean(x * x, axis=-1, keepdims=True) + EPSILON)
        normed = x * inverse
        keep = self.valid[(i * TILE) // (self.rows // MB_CAP)]
        g = self.cot[r, :].astype(F32) * keep
        self.out[r, :] = (normed * self.vec(6) + self.vec(7)).astype(BF)
        self.add_sum(6, g * normed)
        self.add_sum(7, g)
        e = g * self.vec(6)
        e = e - jnp.mean(e, axis=-1, keepdims=True) - normed * jnp.mean(e * normed, axis=-1, keepdims=True)
        e = e * inverse
        self.gs[r, :] = e
        low = e.astype(BF)
        self.gd[r, :] = low
        self.add_sum(5, low.astype(F32))

    def feed_back(self, j, i):
        r = rows_of(i)
        gu = (dot_t(self.gd[r, :], self.w_down[j]) * self.slope[j, r, :].astype(F32)).astype(BF)
        self.slope[j, r, :] = gu
        self.sums[pl.ds(8 + j, 1)] += fold(gu.astype(F32))[None]
        self.gs[r, :] += dot_t(gu, self.w_up[j])

    def feed_grads(self, j, i):
        r = rows_of(i)
        lanes = lanes_of(i, TILE)
        self.w_down[j, r, :] = t_dot(self.active[j, :, lanes], self.gd[...]).astype(BF)
        self.w_up[j, r, :] = t_dot(self.mid[:, lanes], self.slope[j]).astype(BF)

    def first_back(self, i):
        r = rows_of(i)
        g = self.gs[r, :]
        normed = self.normed1[r, :].astype(F32)
        self.add_sum(3, g * normed)
        self.add_sum(4, g)
        e = g * self.vec(3)
        e = e - jnp.mean(e, axis=-1, keepdims=True) - normed * jnp.mean(e * normed, axis=-1, keepdims=True)
        e = e * self.inv1[r, :1]
        self.gs[r, :] = e
        low = e.astype(BF)
        self.gd[r, :] = low
        self.add_sum(2, low.astype(F32))
        self.gctx[r, :] = dot_t(low, self.w_o[...]).astype(BF)

    def out_grad(self, i):
        self.w_o[rows_of(i), :] = t_dot(self.ctx[:, lanes_of(i, TILE)], self.gd[...]).astype(BF)

    def attend_back(self, n):
        s, p = n // self.pairs, n % self.pairs
        masks, lane = self.masks()
        lanes = lanes_of(p)
        rows = rows_of(s, self.seq)
        q, k, v = self.q[rows, lanes], self.k[rows, lanes], self.v[rows, lanes]
        go = self.gctx[rows, lanes]
        prod = go.astype(F32) * self.ctx[rows, lanes].astype(F32)
        lse = self.lse[rows, :]
        chunk = min(TILE, self.seq)
        gq = 0.0
        gks, gvs = [0.0] * (self.seq // chunk), [0.0] * (self.seq // chunk)
        for h in range(2):
            b = 64 * (1 - h)

            def ext(column, one):
                parts = split3(column)
                e = jnp.where(lane == b, one, 0.0)
                for x in range(3):
                    e = jnp.where(lane == b + 1 + x, parts[x], e)
                return e.astype(BF)

            delta = jnp.sum(prod * masks[h].astype(F32), axis=-1, keepdims=True)
            level = jnp.sum(jnp.where(lane == 2 * p + h, lse, 0.0), axis=-1, keepdims=True)
            qh, kh, gh = q * masks[h], k * masks[h], go * masks[h]
            q_ext = qh + ext(level * (-1.0 / self.base), 1.0)
            g_ext = gh + ext(-delta, 0.0)
            k_ext = kh + self.key_ext[s, h]
            v_ext = v * masks[h] + self.key_ext[s, h]
            for c in range(self.seq // chunk):
                part = slice(c * chunk, (c + 1) * chunk)
                probs = jnp.exp2(dot_t(k_ext[part], q_ext) * self.base)
                gs = (probs * dot_t(v_ext[part], g_ext)).astype(BF)
                gvs[c] = gvs[c] + dot(probs.astype(BF), gh)
                gks[c] = gks[c] + dot(gs, qh)
                gq = gq + t_dot(gs, kh[part])
        gq = (gq * self.factor).astype(BF)
        self.q[rows, lanes] = gq
        self.add_sum(0, gq.astype(F32), lanes)
        for c in range(self.seq // chunk):
            r = pl.ds(pl.multiple_of(s * self.seq + c * chunk, chunk), chunk)
            self.k[r, lanes] = (gks[c] * self.factor).astype(BF)
            gv = gvs[c].astype(BF)
            self.v[r, lanes] = gv
            self.add_sum(1, gv.astype(F32), lanes)

    def qkv_grads(self, i):
        x = self.tok[:, lanes_of(i, TILE)].T
        r = rows_of(i)
        for m, g in enumerate((self.q, self.k, self.v)):
            self.g_qkv[m, r, :] = dot(x, g[...]).astype(BF)

    def tokens_grad(self, i):
        r = rows_of(i)
        g = self.gs[r, :] + dot_t(self.q[r, :], self.w_q[...])
        g = g + dot_t(self.k[r, :], self.w_k[...]) + dot_t(self.v[r, :], self.w_v[...])
        self.gtok[r, :] = g.astype(BF)


def loop(n, f):
    lax.fori_loop(0, n, lambda i, c: (f(i), c)[1], 0)


def layer_kernel(
    lens, valid, tok_hbm, cot_hbm, vectors, wq_h, wk_h, wv_h, wo_h, up_h, down_h,
    out_hbm, gtok_hbm, gq_h, gk_h, gv_h, go_h, gup_h, gdown_h, sums_out,
    tok, cot, w_q, w_k, w_v, w_o, w_up, w_down, q, k, v, ctx, normed1, inv1, mid, active, slope,
    gs, gd, lse, key_ext, g_qkv, sums, sems,
):
    copies = [pltpu.make_async_copy(a, b, sems.at[i]) for i, (a, b) in enumerate(
        ((tok_hbm, tok), (wq_h, w_q), (wk_h, w_k), (wv_h, w_v), (wo_h, w_o)))]
    blocks = w_up.shape[0]
    width = tok.shape[1]
    for j in range(blocks):
        copies.append(pltpu.make_async_copy(up_h.at[:, j * width : (j + 1) * width], w_up.at[j], sems.at[5 + j]))
        copies.append(pltpu.make_async_copy(down_h.at[j * width : (j + 1) * width], w_down.at[j], sems.at[9 + j]))
    copies.append(pltpu.make_async_copy(cot_hbm, cot, sems.at[13]))
    for c in copies:
        c.start()
    b = Body(
        lens=lens, valid=valid, tok=tok, cot=cot, vectors=vectors, w_q=w_q, w_k=w_k, w_v=w_v, w_o=w_o,
        w_up=w_up, w_down=w_down, q=q, k=k, v=v, ctx=ctx, normed1=normed1, inv1=inv1, mid=mid, active=active,
        slope=slope, gs=gs, gd=gd, lse=lse, key_ext=key_ext, g_qkv=g_qkv, sums=sums, out=cot, gctx=cot, gtok=tok,
    )
    b.prepare()
    for c in copies[:4]:
        c.wait()
    loop(b.tiles, b.qkv_tile)
    loop(b.seqs * b.pairs, b.attend)
    for c in copies[4:]:
        c.wait()
    loop(b.tiles, b.first_norm)
    loop(blocks * b.tiles, lambda n: b.feed(n // b.tiles, n % b.tiles))
    loop(b.tiles, b.second_norm)
    done = pltpu.make_async_copy(cot, out_hbm, sems.at[0])
    done.start()

    def block(j):
        loop(b.tiles, lambda i: b.feed_back(j, i))
        loop(width // TILE, lambda i: b.feed_grads(j, i))

    loop(blocks, block)
    done.wait()
    loop(b.tiles, b.first_back)
    loop(width // TILE, b.out_grad)
    loop(b.seqs * b.pairs, b.attend_back)
    loop(width // TILE, b.qkv_grads)
    loop(b.tiles, b.tokens_grad)
    sums_out[...] = jnp.sum(sums[...], axis=1)
    outs = [(tok, gtok_hbm), (w_o, go_h), (g_qkv.at[0], gq_h), (g_qkv.at[1], gk_h), (g_qkv.at[2], gv_h)]
    for j in range(blocks):
        outs.append((w_up.at[j], gup_h.at[:, j * width : (j + 1) * width]))
        outs.append((w_down.at[j], gdown_h.at[j * width : (j + 1) * width]))
    copies = [pltpu.make_async_copy(a, o, sems.at[i]) for i, (a, o) in enumerate(outs)]
    for c in copies:
        c.start()
    for c in copies:
        c.wait()


def layer(lens, valid, tok, cot, vectors, w_q, w_k, w_v, w_o, w_up, w_down):
    rows, width = tok.shape
    seqs = lens.shape[0]
    seq = rows // seqs
    ff = w_up.shape[1]
    blocks = ff // width
    any_spec = pl.BlockSpec(memory_space=pl.ANY)
    vm = pl.BlockSpec(memory_space=pltpu.VMEM)
    sm = pl.BlockSpec(memory_space=pltpu.SMEM)
    square = pltpu.VMEM((width, width), BF)
    act = pltpu.VMEM((rows, width), BF)
    shape = jax.ShapeDtypeStruct
    sq = shape((width, width), BF)
    return pl.pallas_call(
        layer_kernel,
        out_shape=(shape(tok.shape, BF), shape(tok.shape, BF), sq, sq, sq, sq,
                   shape(w_up.shape, BF), shape(w_down.shape, BF), shape((16, width), F32)),
        in_specs=[sm, sm, any_spec, any_spec, vm] + [any_spec] * 6,
        out_specs=(any_spec,) * 8 + (vm,),
        scratch_shapes=[
            act, act, square, square, square, square,
            pltpu.VMEM((blocks, width, width), BF), pltpu.VMEM((blocks, width, width), BF),
            act, act, act, act, act, pltpu.VMEM((rows, 128), F32), act,
            pltpu.VMEM((blocks, rows, width), BF), pltpu.VMEM((blocks, rows, width), BF),
            pltpu.VMEM((rows, width), F32), act, pltpu.VMEM((rows, 128), F32),
            pltpu.VMEM((seqs, 2, seq, 128), BF), pltpu.VMEM((3, width, width), BF),
            pltpu.VMEM((16, 8, width), F32), pltpu.SemaphoreType.DMA((16,)),
        ],
        compiler_params=pltpu.CompilerParams(vmem_limit_bytes=67043328),
    )(lens, valid, tok, cot, vectors, w_q, w_k, w_v, w_o, w_up, w_down)


def local(tokens, cotangent, lengths, mb_count, query_weight, query_bias, key_weight, value_weight, value_bias,
          output_weight, output_bias, first_gain, first_shift, up_weight, up_bias, down_weight, down_bias,
          second_gain, second_shift):
    width = tokens.shape[1]
    group_count = mb_count[lax.axis_index("dp")]
    valid = (jnp.arange(MB_CAP, dtype=jnp.int32) < group_count).astype(F32)

    def gather(x):
        return lax.all_gather(x, "fsdp", axis=0, tiled=True)

    small = (query_bias, value_bias, output_bias, first_gain, first_shift, down_bias, second_gain, second_shift)
    packed = gather(jnp.stack(small, axis=1))
    ups = gather(up_bias).reshape(-1, width)
    vectors = jnp.concatenate([packed.T, ups, jnp.zeros((8 - ups.shape[0], width), BF)], axis=0).astype(F32)
    weights = [gather(w) for w in (query_weight, key_weight, value_weight, output_weight, up_weight, down_weight)]
    res = layer(lengths, valid, tokens, cotangent, vectors, *weights)
    out, gtok, grads, sums = res[0], res[1], res[2:8], res[8]

    def reduce(x):
        y = lax.psum_scatter(x, "fsdp", scatter_dimension=0, tiled=True)
        return lax.psum(y, "dp").astype(F32)

    gq, gk, gv, go, gup, gdown = [reduce(g) for g in grads]
    total = lax.psum(sums, ("dp", "fsdp"))
    here = lax.axis_index("fsdp")

    def piece(x, n):
        return lax.dynamic_slice_in_dim(x, here * n, n, 0)

    part = [piece(total[i], query_bias.shape[0]) for i in range(8)]
    up_part = piece(total[8 : 8 + ups.shape[0]].reshape(-1), up_bias.shape[0])
    return (out, gtok, gq, part[0], gk, gv, part[1], go, part[2], part[3], part[4], gup, up_part, gdown,
            part[5], part[6], part[7])


def solution(mesh):
    row, shard, vector = P(("dp", "fsdp"), None), P("fsdp", None), P("fsdp")
    return jax.shard_map(
        local,
        mesh=mesh,
        in_specs=(row, row, P(("dp", "fsdp")), P(), shard, vector, shard, shard, vector, shard, vector, vector,
                  vector, shard, vector, shard, vector, vector, vector),
        out_specs=(row, row, shard, vector, shard, shard, vector, shard, vector, vector, vector, shard, vector,
                   shard, vector, vector, vector),
        check_vma=False,
    )
```

time: 775 us -> 654 us (0.84); the launches traced: 764 us -> 654 us
  matrix products: 156 us -> 0 us
  Pallas kernels: 0 us -> 119 us
  local copies, waits for them, and re-layouts: 47.2 us -> 3.93 us
  waiting for transfers between devices: 406 us -> 443 us
  other arithmetic: 44.7 us -> 8.16 us
  blocking collectives: 80.1 us -> 65.8 us
  loops' own time: 9.85 us -> 0 us
    dot_general x33 -> x0, matrix products: 156 us -> none  [the longest x12 65.3 us: project(): return jnp.dot(left, right, preferred_element_type=jnp.float32)]
    pallas_call x0 -> x1, Pallas kernels: none -> 119 us  [layer(): pl.pallas_call(layer_kernel, out_shape=(shape(tok.shape, BF), shape(tok.s...]
    all_gather x6, waiting for transfers between devices: 72.5 us -> 170 us  [gather(): return lax.all_gather(x, 'fsdp', axis=0, tiled=True)]
    reduce_scatter x6, waiting for transfers between devices: 310 us -> 241 us  [reduce(): y = lax.psum_scatter(x, 'fsdp', scatter_dimension=0, tiled=True)]
    unnamed x2 -> x0, blocking collectives: 57.4 us -> none
    psum x1, blocking collectives: 10 us -> 38.5 us  [local(): total = lax.psum(sums, ('dp', 'fsdp'))]
    cond x48 -> x0, local copies, waits for them, and re-layouts: 26.2 us -> none  [the longest x6 24.9 us: local(): lax.cond(slot_index < group_count, run_backward, skip_backward, totals)]
    convert_element_type x39 -> x8, other arithmetic: 29.4 us -> 8.12 us  [the longest x6 6.27 us: reduce(): return lax.psum(y, 'dp').astype(F32)]
  transfers between devices with their start and end apart: 13 -> 13, of which waited for: 11 -> 12; matrix products, arithmetic and copies ran while one was open for 15% -> 1% of each run, Pallas kernels for 0% -> 0%
where the time goes in v1:
time: 654 us
  waiting for transfers between devices  443 us (68%)
  Pallas kernels  119 us (18%)
  blocking collectives  65.8 us (10%)
  between operations  14.2 us (2%)
  other arithmetic  8.16 us (1%)
    reduce_scatter x6, waiting for transfers between devices, reduce(): y = lax.psum_scatter(x, 'fsdp', scatter_dimension=0, tiled=True)  241 us
    all_gather x6, waiting for transfers between devices, gather(): return lax.all_gather(x, 'fsdp', axis=0, tiled=True)  170 us
    pallas_call x1, Pallas kernels, layer(): pl.pallas_call(layer_kernel, out_shape=(shape(tok.shape, BF), shape(tok.s...  119 us
    psum x1, blocking collectives, local(): total = lax.psum(sums, ('dp', 'fsdp'))  38.5 us
    all_gather x2, blocking collectives, gather(): return lax.all_gather(x, 'fsdp', axis=0, tiled=True)  27.3 us
    psum x1, waiting for transfers between devices, reduce(): return lax.psum(y, 'dp').astype(F32)  25.3 us
  transfers between devices with their start and end apart: 13, of which 12 were waited for; matrix products, arithmetic and copies ran while one was open for 1% of the time, Pallas kernels for 0%

profile of v1, /device:TPU:0, one launch (start us, length us, event | category | flops | bytes accessed | tf_op | source)
XLA Modules:
  0.0 654.1 jit_solution(5498785206345990726)
XLA Ops:
  11.4 14.5 %all-gather = bf16[8,96,8]{1,2,0:T(8,128)(2,1)S(1)} all-gather(bf16[1,96,8]{1,2,0:T(8,128)(2,1)S(1)} %bitcast.30), channel_id=1, replica_groups=mesh['dp'=4,'fsdp'=8] {'fsdp'}, dimensions={0}, use_global_device_ids=true | all-gather | bytes 13824 | tf_op jit(solution)/shard_map/all_gather | solution.py:346
  26.0 12.8 %all-gather.1 = bf16[8,1,384]{2,1,0:T(2,128)(2,1)S(1)} all-gather(bf16[1,1,384]{2,1,0:T(2,128)(2,1)S(1)} %reshape.52), channel_id=1, replica_groups=mesh['dp'=4,'fsdp'=8] {'fsdp'}, dimensions={0}, use_global_device_ids=true | all-gather | bytes 6912 | tf_op jit(solution)/shard_map/all_gather | solution.py:346
  39.6 1.2 compare_convert_fusion.valid
  41.4 18.0 %all-gather.13.cloned.1.call-done.wv_h = bf16[768,768]{1,0:T(8,128)(2,1)} async-done(((bf16[96,768]{1,0:T(8,128)(2,1)}), bf16[768,768]{1,0:T(8,128)(2,1)}) %all-gather.13.cloned.1.call-update) | async-done | bytes 1179664 | tf_op jit(solution)/shard_map/all_gather | solution.py:346
  59.4 24.1 %all-gather.15.cloned.1.call-done.wo_h = bf16[768,768]{1,0:T(8,128)(2,1)} async-done(((bf16[96,768]{1,0:T(8,128)(2,1)}), bf16[768,768]{1,0:T(8,128)(2,1)}) %all-gather.15.cloned.1.call-update) | async-done | bytes 1179664 | tf_op jit(solution)/shard_map/all_gather | solution.py:346
  83.5 24.0 %all-gather.9.cloned.1.call-done.wq_h = bf16[768,768]{1,0:T(8,128)(2,1)} async-done(((bf16[96,768]{1,0:T(8,128)(2,1)}), bf16[768,768]{1,0:T(8,128)(2,1)}) %all-gather.9.cloned.1.call-update) | async-done | bytes 1179664 | tf_op jit(solution)/shard_map/all_gather | solution.py:346
  107.5 52.4 %all-gather.17.cloned.1.call-done.up_h = bf16[768,3072]{1,0:T(8,128)(2,1)} async-done(((bf16[96,3072]{1,0:T(8,128)(2,1)}), bf16[768,3072]{1,0:T(8,128)(2,1)}) %all-gather.17.cloned.1.call-update) | async-done | bytes 4718608 | tf_op jit(solution)/shard_map/all_gather | solution.py:346
  159.8 51.5 %all-gather.19.cloned.1.call-done.down_h = bf16[3072,768]{1,0:T(8,128)(2,1)} async-done(((bf16[384,768]{1,0:T(8,128)(2,1)}), bf16[3072,768]{1,0:T(8,128)(2,1)}) %all-gather.19.cloned.1.call-update) | async-done | bytes 4718608 | tf_op jit(solution)/shard_map/all_gather | solution.py:346
  211.3 118.7 %shard_map.314 = (bf16[1024,768]{1,0:T(8,128)(2,1)}, bf16[1024,768]{1,0:T(8,128)(2,1)}, bf16[768,768]{1,0:T(8,128)(2,1)}, bf16[768,768]{1,0:T(8,128)(2,1)}, bf16...) custom-call(s32[2]{0:T(128)} %lens.1, ...), custom_call_target="tpu_custom_call" | custom-call | tf_op jit(solution)/shard_map/pallas_call | solution.py:319
  330.1 0.7 reduce-scatter.13.cloned.1.call-update
  333.5 28.5 %reduce-scatter.11.cloned.1.call-done = bf16[96,768]{1,0:T(8,128)(2,1)} async-done(((bf16[768,768]{1,0:T(8,128)(2,1)}), bf16[96,768]{1,0:T(8,128)(2,1)}) %reduce-scatter.11.cloned.1.call-update) | async-done | bytes 147472 | tf_op jit(solution)/shard_map/reduce_scatter | solution.py:357
  362.0 33.4 %reduce-scatter.13.cloned.1.call-done = bf16[96,768]{1,0:T(8,128)(2,1)} async-done(((bf16[768,768]{1,0:T(8,128)(2,1)}), bf16[96,768]{1,0:T(8,128)(2,1)}) %reduce-scatter.13.cloned.1.call-update) | async-done | bytes 147472 | tf_op jit(solution)/shard_map/reduce_scatter | solution.py:357
  395.3 34.1 %reduce-scatter.7.cloned.1.call-done = bf16[96,768]{1,0:T(8,128)(2,1)} async-done(((bf16[768,768]{1,0:T(8,128)(2,1)}), bf16[96,768]{1,0:T(8,128)(2,1)}) %reduce-scatter.7.cloned.1.call-update) | async-done | bytes 147472 | tf_op jit(solution)/shard_map/reduce_scatter | solution.py:357
  429.5 33.9 %reduce-scatter.9.cloned.1.call-done = bf16[96,768]{1,0:T(8,128)(2,1)} async-done(((bf16[768,768]{1,0:T(8,128)(2,1)}), bf16[96,768]{1,0:T(8,128)(2,1)}) %reduce-scatter.9.cloned.1.call-update) | async-done | bytes 147472 | tf_op jit(solution)/shard_map/reduce_scatter | solution.py:357
  463.4 55.4 %reduce-scatter.15.cloned.1.call-done = bf16[96,3072]{1,0:T(8,128)(2,1)} async-done(((bf16[768,3072]{1,0:T(8,128)(2,1)}), bf16[96,3072]{1,0:T(8,128)(2,1)}) %reduce-scatter.15.cloned.1.call-update) | async-done | bytes 589840 | tf_op jit(solution)/shard_map/reduce_scatter | solution.py:357
  518.8 55.5 %reduce-scatter.17.cloned.1.call-done = bf16[384,768]{1,0:T(8,128)(2,1)} async-done(((bf16[3072,768]{1,0:T(8,128)(2,1)}), bf16[384,768]{1,0:T(8,128)(2,1)}) %reduce-scatter.17.cloned.1.call-update) | async-done | bytes 589840 | tf_op jit(solution)/shard_map/reduce_scatter | solution.py:357
  574.4 38.5 %psum.50 = f32[16,768]{1,0:T(8,128)S(1)} all-reduce(f32[16,768]{1,0:T(8,128)S(1)} %copy-done.5), channel_id=1, replica_groups=mesh['dp'=4,'fsdp'=8] {'dp','fsdp'}, use_global_device_ids=true, to_apply=%region_2.0 | all-reduce | flops 12288 | bytes 98304 | tf_op jit(solution)/shard_map/psum | solution.py:361
  615.9 25.3 %all-reduce.3.cloned.1.call-done = (bf16[96,768]{1,0:T(8,128)(2,1)}, bf16[96,768]{1,0:T(8,128)(2,1)}, bf16[96,768]{1,0:T(8,128)(2,1)}, bf16[96,768]{1,0:T(8,128)...) async-done(((bf16[96,768]{1,0:T(8,128)(2,1)}, bf16[96,768]{1,0:T(8,128)(2,1)}, bf16[96,768]{1,0:T(8,128)(2,1)}, bf16[96,768]{1,0:T(8,128)(2,1)}, ...) | async-done | bytes 1769488 | tf_op jit(solution)/shard_map/psum | solution.py:358
  641.2 2.2 convert_element_type.30
  643.5 1.1 convert_element_type.31
  644.6 0.7 convert_element_type.26
  645.3 0.7 convert_element_type.27
  646.1 0.7 convert_element_type.28
  646.8 0.7 convert_element_type.29
  (76 shorter events, 11.3 us)
Async XLA Ops:
  7.2 4.1 copy-start.7
  7.2 4.1 copy-start.8
  7.2 4.1 copy-start.9
  7.2 4.1 copy-start.10
  7.2 4.1 copy-start.11
  7.2 4.1 copy-start.12
  7.3 4.1 copy-start.13
  7.3 4.1 copy-start.14
  7.3 18.7 %copy-start.6 = (bf16[384]{0:T(512)(128)(2,1)S(1)}, bf16[384]{0:T(512)(128)(2,1)}, u32[]{:S(2)}) copy-start(bf16[384]{0:T(512)(128)(2,1)} %param.33) | copy-start | bytes 2308
  7.3 31.6 %copy-start.15 = (s32[4]{0:T(128)S(1)}, s32[4]{0:T(128)}, u32[]{:S(2)}) copy-start(s32[4]{0:T(128)} %param.22) | copy-start | bytes 52
  7.3 34.1 %all-gather.11.cloned.1.call-start = ((), (), s32[]{:S(2)}) async-start(), calls=%async_computation.7 | async-start | bytes 1327104 | tf_op jit(solution)/shard_map/all_gather | solution.py:346
  8.0 51.4 %all-gather.13.cloned.1.call-start = ((), (), s32[]{:S(2)}) async-start(), calls=%async_computation.8 | async-start | bytes 1327104 | tf_op jit(solution)/shard_map/all_gather | solution.py:346
  8.8 74.7 %all-gather.15.cloned.1.call-start = ((), (), s32[]{:S(2)}) async-start(), calls=%async_computation.9 | async-start | bytes 1327104 | tf_op jit(solution)/shard_map/all_gather | solution.py:346
  9.5 98.0 %all-gather.9.cloned.1.call-start = ((), (), s32[]{:S(2)}) async-start(), calls=%async_computation.6 | async-start | bytes 1327104 | tf_op jit(solution)/shard_map/all_gather | solution.py:346
  10.1 149.8 %all-gather.17.cloned.1.call-start = ((), (), s32[]{:S(2)}) async-start(), calls=%async_computation.10 | async-start | bytes 5308416 | tf_op jit(solution)/shard_map/all_gather | solution.py:346
  10.7 200.7 %all-gather.19.cloned.1.call-start = ((), (), s32[]{:S(2)}) async-start(), calls=%async_computation.11 | async-start | bytes 5308416 | tf_op jit(solution)/shard_map/all_gather | solution.py:346
  11.3 350.7 %reduce-scatter.11.cloned.1.call-start = ((), (), s32[]{:S(2)}) async-start(), calls=%async_computation.14 | async-start | bytes 1327104 | tf_op jit(solution)/shard_map/reduce_scatter | solution.py:357
  330.1 65.3 %reduce-scatter.13.cloned.1.call-start = ((), (), s32[]{:S(2)}) async-start(), calls=%async_computation.15 | async-start | bytes 1327104 | tf_op jit(solution)/shard_map/reduce_scatter | solution.py:357
  330.8 98.6 %reduce-scatter.7.cloned.1.call-start = ((), (), s32[]{:S(2)}) async-start(), calls=%async_computation.12 | async-start | bytes 1327104 | tf_op jit(solution)/shard_map/reduce_scatter | solution.py:357
  331.6 131.9 %reduce-scatter.9.cloned.1.call-start = ((), (), s32[]{:S(2)}) async-start(), calls=%async_computation.13 | async-start | bytes 1327104 | tf_op jit(solution)/shard_map/reduce_scatter | solution.py:357
  332.1 186.7 %reduce-scatter.15.cloned.1.call-start = ((), (), s32[]{:S(2)}) async-start(), calls=%async_computation.16 | async-start | bytes 5308416 | tf_op jit(solution)/shard_map/reduce_scatter | solution.py:357
  332.9 241.4 %reduce-scatter.17.cloned.1.call-start = ((), (), s32[]{:S(2)}) async-start(), calls=%async_computation.17 | async-start | bytes 5308416 | tf_op jit(solution)/shard_map/reduce_scatter | solution.py:357
  333.5 240.9 %copy-start.5 = (f32[16,768]{1,0:T(8,128)S(1)}, f32[16,768]{1,0:T(8,128)}, u32[]{:S(2)}) copy-start(f32[16,768]{1,0:T(8,128)} %get-tuple-element.29) | copy-start | bytes 147460
  333.5 307.8 %all-reduce.3.cloned.1.call-start = ((), (), s32[]{:S(2)}) async-start(), calls=%async_computation.18 | async-start | bytes 3538944 | tf_op jit(solution)/shard_map/psum | solution.py:358
  (5 other events, 11.1 us)
Sparse Core Ops, SparseCore 0:
  9.7 25.5 all-gather.10
  37.0 22.3 all-gather.12
  61.1 22.4 all-gather.14
  85.0 22.4 all-gather.8
  109.0 50.8 all-gather.16
  161.3 49.9 all-gather.18
  330.2 31.7 reduce-scatter.10
  364.2 31.0 reduce-scatter.12
  398.2 31.2 reduce-scatter.6
  432.2 31.1 reduce-scatter.8
  465.7 53.0 reduce-scatter.14
  521.0 53.3 reduce-scatter.16
  578.1 63.0 all-reduce.2
